TPU v7x, 32 devices: a whole 2x2x4 slice. The times are simulated.
32 devices in a mesh: dp: 8 (over y, x, core), mp: 4 (over z).
Axes of the slice: x: 2, y: 2, z: 4, core: 2. Of those that a mesh axis runs over, the one named last changes fastest.
Arguments:
- hidden_rows: bfloat16 [4096, 3584], P('dp'), may hold values from -6 to 6
- key_grad: bfloat16 [4096, 512], P('dp', 'mp'), may hold values from -6 to 6
- value_grad: bfloat16 [4096, 512], P('dp', 'mp'), may hold values from -6 to 6
- visual_rows: bfloat16 [2048, 1024], P('dp'), may hold values from -6 to 6
- visual_cotangent: bfloat16 [8, 4, 64, 3584], P('dp'), may hold values from -6 to 6
- norm_gain: float32 [1024], replicated, may hold values from 0.25 to 1.75
- norm_bias: float32 [1024], replicated, may hold values from -3 to 3
- fc1_weight: bfloat16 [1024, 4096], P(None, 'mp'), may hold values from -0.1875 to 0.1875
- fc1_bias: float32 [4096], P('mp'), may hold values from -3 to 3
- fc2_weight: bfloat16 [4096, 1024], P('mp'), may hold values from -0.09375 to 0.09375
- fc2_bias: float32 [1024], replicated, may hold values from -3 to 3
- layer_scale: float32 [1024], replicated, may hold values from 0.3 to 1.5
- token_counts: int32 [8, 8], P('dp'), may hold values from 1 to 32, as said below
- dest_offsets: int32 [8, 8], P('dp'), may hold values from 1 to 4, as said below
Outputs:
- key_weight_grad: float32 [3592, 512], P('dp', 'mp')
- value_weight_grad: float32 [3592, 512], P('dp', 'mp')
- projector_grad: float32 [3592, 1024], P('dp', 'mp')
- handoff: bfloat16 [8, 4, 64, 1024], P('dp', None, None, 'mp')
Inputs may be any that keep to these rules, and one draw needn't show every extreme that they name: `token_counts`: on every data rank the images of one distance, chosen per rank, all have 32 rows. `dest_offsets`: every data rank sends exactly 2 images to each distance from 1 to 4.
All inputs are finite; a program needn't handle non-finite values.
Results may differ from a plain program's by a relative error of at most 0.0046.
Values may be sent and summed in bfloat16 or wider, within the bound.
A program may use at most 64 MiB of HBM per device.

v0:
```python
import jax
import jax.numpy as jnp
from jax import lax
from jax.sharding import PartitionSpec as P

SPREAD = 4
CAP = 64


def shifted(x, axis, by):
    count = lax.axis_size(axis)
    return lax.ppermute(x, axis, [(i, (i + by) % count) for i in range(count)])


def pack_rows(rows, counts, offsets):
    total_rows = rows.shape[0]
    images = counts.shape[0]
    ends = jnp.cumsum(counts)
    starts = ends - counts
    places = jnp.arange(total_rows)
    image_ids = jnp.arange(images)
    owner = jnp.sum((places[:, None] >= ends[None, :]).astype(jnp.int32), axis=1)
    member = (owner[:, None] == image_ids[None, :]).astype(jnp.int32)
    earlier = (image_ids[None, :] < image_ids[:, None]) & (offsets[None, :] == offsets[:, None])
    before = jnp.sum(earlier.astype(jnp.int32) * counts[None, :], axis=1)
    row_dest = jnp.sum(member * offsets[None, :], axis=1)
    row_start = jnp.sum(member * starts[None, :], axis=1)
    row_before = jnp.sum(member * before[None, :], axis=1)
    slot_index = row_before + places - row_start
    target = jnp.where(places < ends[images - 1], (row_dest - 1) * CAP + slot_index, -1)
    slot_ids = jnp.arange(SPREAD * CAP)
    select = (slot_ids[:, None] == target[None, :]).astype(jnp.bfloat16)
    packed = jnp.dot(select, rows, preferred_element_type=jnp.float32).astype(jnp.bfloat16)
    return packed.reshape(SPREAD, CAP, rows.shape[1])


def vision(
    visual_rows,
    norm_gain,
    norm_bias,
    fc1_weight,
    fc1_bias,
    fc2_weight,
    fc2_bias,
    layer_scale,
    token_counts,
    dest_offsets,
):
    values = visual_rows.astype(jnp.float32)
    center = jnp.mean(values, axis=1, keepdims=True)
    spread_sq = jnp.mean((values - center) ** 2, axis=1, keepdims=True)
    normed = ((values - center) * lax.rsqrt(spread_sq + 1e-06) * norm_gain + norm_bias).astype(
        jnp.bfloat16
    )
    hidden = jax.nn.gelu(
        jnp.dot(normed, fc1_weight, preferred_element_type=jnp.float32) + fc1_bias,
        approximate=False,
    ).astype(jnp.bfloat16)
    partial_value = jnp.dot(hidden, fc2_weight, preferred_element_type=jnp.float32)
    summed = lax.psum_scatter(partial_value, "mp", scatter_dimension=1, tiled=True)
    column_count = summed.shape[1]
    first_col = lax.axis_index("mp") * column_count
    own_values = lax.dynamic_slice_in_dim(values, first_col, column_count, 1)
    own_scale = lax.dynamic_slice_in_dim(layer_scale, first_col, column_count, 0)
    own_bias = lax.dynamic_slice_in_dim(fc2_bias, first_col, column_count, 0)
    encoded = (own_values + own_scale * (summed + own_bias)).astype(jnp.bfloat16)
    packed = pack_rows(encoded, token_counts[0], dest_offsets[0])
    received = []
    for distance in range(SPREAD):
        received.append(shifted(packed[distance], "dp", distance + 1))
    return jnp.stack(received, axis=0)[None]


def per_device(
    hidden_rows,
    key_grad,
    value_grad,
    visual_rows,
    visual_cotangent,
    norm_gain,
    norm_bias,
    fc1_weight,
    fc1_bias,
    fc2_weight,
    fc2_bias,
    layer_scale,
    token_counts,
    dest_offsets,
):
    tokens_here, width = hidden_rows.shape
    devices = lax.axis_size("dp")
    shard_rows = (width + devices) // devices
    padded_width = shard_rows * devices
    ones_column = jnp.ones((tokens_here, 1), jnp.bfloat16)
    zero_columns = jnp.zeros((tokens_here, padded_width - width - 1), jnp.bfloat16)
    augmented = jnp.concatenate([hidden_rows, ones_column, zero_columns], axis=1)
    key_cols = key_grad.shape[1]
    kv_cotangent = jnp.concatenate([key_grad, value_grad], axis=1)

    def make_projector(handoff):
        slot_count = handoff.shape[1] * handoff.shape[2]
        cot_flat = visual_cotangent.reshape(slot_count, width)
        cot_padded = jnp.concatenate(
            [cot_flat, jnp.zeros((slot_count, padded_width - width), jnp.bfloat16)], axis=1
        )
        received_rows = handoff.reshape(slot_count, handoff.shape[3])

        def projector_rows(start, count):
            return lax.dot_general(
                cot_padded,
                received_rows,
                (((0,), (0,)), ((), ())),
                preferred_element_type=jnp.float32,
            )

        return projector_rows

    kv_results = lax.psum_scatter(
        lax.dot_general(
            augmented, kv_cotangent, (((0,), (0,)), ((), ())), preferred_element_type=jnp.float32
        ),
        "dp",
        scatter_dimension=0,
        tiled=True,
    )
    key_weight_grad = kv_results[:, :key_cols]
    value_weight_grad = kv_results[:, key_cols:]
    handoff = vision(
        visual_rows,
        norm_gain,
        norm_bias,
        fc1_weight,
        fc1_bias,
        fc2_weight,
        fc2_bias,
        layer_scale,
        token_counts,
        dest_offsets,
    )
    projector_rows = make_projector(handoff)
    projector_grad = lax.psum_scatter(
        projector_rows(jnp.int32(0), lax.axis_size("dp") * shard_rows),
        "dp",
        scatter_dimension=0,
        tiled=True,
    )
    return (key_weight_grad, value_weight_grad, projector_grad, handoff)


def solution(mesh):
    placed = (
        P("dp", None),
        P("dp", "mp"),
        P("dp", "mp"),
        P("dp", None),
        P("dp", None, None, None),
        P(),
        P(),
        P(None, "mp"),
        P("mp"),
        P("mp", None),
        P(),
        P(),
        P("dp", None),
        P("dp", None),
    )
    return jax.shard_map(
        per_device,
        mesh=mesh,
        in_specs=placed,
        out_specs=(P("dp", "mp"), P("dp", "mp"), P("dp", "mp"), P("dp", None, None, "mp")),
        check_vma=False,
    )
```

profile of v0, /device:TPU:1, one launch (start us, length us, event | category | flops | bytes accessed | tf_op | source)
XLA Modules:
  0.0 157.3 jit_solution(14281039852675778282)
XLA Ops:
  8.0 0.0 reduce-scatter.4.cloned.1.call-start
  8.1 1.3 convert_reduce_fusion
  9.4 1.3 multiply_reduce_fusion
  10.8 6.3 %fusion.13 = f32[256,1024]{1,0:T(8,128)} fusion(bf16[1024,1024]{1,0:T(8,128)(2,1)S(1)} %copy-done, bf16[1024,1024]{1,0:T(8,128)(2,1)} %param.21, bf16[256,1024]{1,0:T(8,128)(2,1)} %param.17, f32[1024]{0:T(1024)} %param.22, f32[1024]{0:T(1024)} %param.20, f32[1024]{0:T(1024)} %param.19, f32[256]{0:T(256)S(1)} %add_rsqrt_fusion, ...), kind=kOutput, calls=%fused_computation.25 | convolution fusion | flops 1092616192 | bytes 5781504 | tf_op jit(solution)/shard_map/dot_general | solution.py:59
  17.1 0.0 all-reduce.6.cloned.1.call-start
  17.1 1.1 convert_element_type.22
  18.3 0.8 dynamic_slice.11
  19.0 0.8 dynamic_slice.10
  19.8 0.2 reduce-window.4
  20.0 0.6 slice.28
  20.7 6.6 %concatenate.9 = bf16[512,3592]{1,0:T(8,128)(2,1)} concatenate(bf16[512,3584]{1,0:T(8,128)(2,1)} %param.14, bf16[512,1]{1,0:T(8,128)(2,1)S(1)} %broadcast_in_dim.7, bf16[512,7]{1,0:T(8,128)(2,1)S(1)} %broadcast_in_dim.8), dimensions={1} | concatenate | bytes 7356416 | tf_op jit(solution)/shard_map/concatenate | solution.py:96
  27.3 0.1 convert_reduce_fusion.1
  27.4 0.2 select_reduce_fusion.3
  27.6 0.1 select_reduce_fusion.2
  27.6 0.7 compare_select_fusion
  28.3 17.9 %reduce-scatter.4.cloned.1.call-done = f32[256,256]{1,0:T(8,128)} async-done(((f32[256,1024]{1,0:T(8,128)}), f32[256,256]{1,0:T(8,128)}) %reduce-scatter.4.cloned.1.call-update) | async-done | bytes 262160 | tf_op jit(solution)/shard_map/reduce_scatter | solution.py:60
  46.2 1.2 convolution_convert_fusion
  47.5 1.3 collective-permute-start.3
  48.7 1.5 collective-permute-start.2
  50.2 1.2 collective-permute-start.1
  51.4 0.5 collective-permute-start
  51.9 5.1 %fusion.53 = f32[3592,256]{1,0:T(8,128)} fusion(bf16[512,3592]{1,0:T(8,128)(2,1)} %concatenate.9, bf16[512,128]{1,0:T(8,128)(2,1)S(1)} %copy-done.2, bf16[512,128]{1,0:T(8,128)(2,1)S(1)} %copy-done.3), kind=kOutput, calls=%fused_computation.62 | convolution fusion | flops 942145536 | bytes 7618560 | tf_op jit(solution)/shard_map/dot_general | solution.py:119
  57.0 0.6 copy-done.5
  57.6 0.6 fusion.98
  59.6 0.7 fusion.95
  60.2 4.4 %fusion.1 = f32[3592,256]{1,0:T(8,128)} fusion(bf16[256,256]{1,0:T(8,128)(2,1)S(1)} %bitcast.27, bf16[256,3584]{1,0:T(8,128)(2,1)} %bitcast.26), kind=kOutput, calls=%fused_computation | convolution fusion | flops 470810624 | bytes 5644288 | tf_op jit(solution)/shard_map/dot_general | solution.py:109
  64.6 53.1 %fusion = f32[456,256]{1,0:T(8,128)S(1)} fusion(f32[3592,256]{1,0:T(8,128)} %fusion.1), kind=kCustom, calls=%all-reduce-scatter | all-reduce-scatter fusion | flops 933889 | bytes 4145664
  117.7 4.4 %collective-permute-start.4 = (f32[49,256]{1,0:T(8,128)S(1)}, f32[49,256]{1,0:T(8,128)S(1)}, u32[]{:S(2)}, u32[]{:S(2)}) collective-permute-start(f32[49,256]{1,0:T(8,128)S(1)} %slice.37), channel_id=1, source_target_pairs={{0,4},{4,8},{8,12},{12,16},{16,20},{20,24},{24,28},{1,5},{5,9},{9,... | collective-permute-start | bytes 150536
  122.1 24.5 %all-reduce.6.cloned.1.call-done = f32[3592,256]{1,0:T(8,128)} async-done(((f32[3592,256]{1,0:T(8,128)}), f32[3592,256]{1,0:T(8,128)}) %all-reduce.6.cloned.1.call-update) | async-done | bytes 3678224
  146.6 1.9 %fusion.96 = (f32[449,128]{1,0:T(8,128)}, f32[449,128]{1,0:T(8,128)}) fusion(f32[3592,256]{1,0:T(8,128)} %all-reduce.6.cloned.1.call-done, u32[]{:T(128)S(6)} %multiply.13, u32[]{:T(128)S(6)} %convert), kind=kLoop, calls=%fused_computation.122 | loop fusion | bytes 919560 | tf_op jit(solution)/shard_map/slice | solution.py:127
  148.5 0.5 concatenate.12
  149.0 0.8 constant_dynamic-slice_fusion
  (27 shorter events, 0.2 us)
Async XLA Ops:
  8.0 2.7 %copy-start = (bf16[1024,1024]{1,0:T(8,128)(2,1)S(1)}, bf16[1024,1024]{1,0:T(8,128)(2,1)}, u32[]{:S(2)}) copy-start(bf16[1024,1024]{1,0:T(8,128)(2,1)} %param.23) | copy-start | bytes 6291460
  8.0 38.2 %reduce-scatter.4.cloned.1.call-start = ((), (), s32[]{:S(2)}) async-start(), calls=%async_computation.1 | async-start | bytes 1310720 | tf_op jit(solution)/shard_map/reduce_scatter | solution.py:60
  10.7 6.4 %copy-start.1 = (bf16[256,1024]{1,0:T(8,128)(2,1)S(1)}, bf16[256,1024]{1,0:T(8,128)(2,1)}, u32[]{:S(2)}) copy-start(bf16[256,1024]{1,0:T(8,128)(2,1)} %param.17) | copy-start | bytes 1572868
  10.8 9.0 %copy-start.6 = (s32[1,8]{1,0:T(1,128)S(1)}, s32[1,8]{1,0:T(1,128)}, u32[]{:S(2)}) copy-start(s32[1,8]{1,0:T(1,128)} %param.26) | copy-start | bytes 100
  17.1 129.6 %all-reduce.6.cloned.1.call-start = ((), (), s32[]{:S(2)}) async-start(), calls=%async_computation.2 | async-start | bytes 7356416
  20.6 6.8 %copy-start.4 = (s32[1,8]{1,0:T(1,128)S(1)}, s32[1,8]{1,0:T(1,128)}, u32[]{:S(2)}) copy-start(s32[1,8]{1,0:T(1,128)} %param.27) | copy-start | bytes 100
  20.6 31.3 %copy-start.2 = (bf16[512,128]{1,0:T(8,128)(2,1)S(1)}, bf16[512,128]{1,0:T(8,128)(2,1)}, u32[]{:S(2)}) copy-start(bf16[512,128]{1,0:T(8,128)(2,1)} %param.16) | copy-start | bytes 393220
  20.6 31.3 %copy-start.3 = (bf16[512,128]{1,0:T(8,128)(2,1)S(1)}, bf16[512,128]{1,0:T(8,128)(2,1)}, u32[]{:S(2)}) copy-start(bf16[512,128]{1,0:T(8,128)(2,1)} %param.15) | copy-start | bytes 393220
  47.5 12.1 %collective-permute-start.3 = (bf16[64,256]{1,0:T(8,128)(2,1)S(1)}, bf16[64,256]{1,0:T(8,128)(2,1)S(1)}, u32[]{:S(2)}, u32[]{:S(2)}) collective-permute-start(bf16[64,256]{1,0:T(8,128)(2,1)S(1)} %get-tuple-element.12), channel_id=1, source_target_pairs={{0,16},{4,20},{8,24},{12,28},{16,0},{20,4},{24,8},{28,12},{1,17},{... | collective-permute-start | bytes 98312 | tf_op jit(solution)/shard_map/ppermute | solution.py:12
  48.7 10.8 %collective-permute-start.2 = (bf16[64,256]{1,0:T(8,128)(2,1)S(1)}, bf16[64,256]{1,0:T(8,128)(2,1)S(1)}, u32[]{:S(2)}, u32[]{:S(2)}) collective-permute-start(bf16[64,256]{1,0:T(8,128)(2,1)S(1)} %get-tuple-element.13), channel_id=1, source_target_pairs={{0,12},{4,16},{8,20},{12,24},{16,28},{20,0},{24,4},{28,8},{1,13},{... | collective-permute-start | bytes 98312 | tf_op jit(solution)/shard_map/ppermute | solution.py:12
  50.2 9.3 %collective-permute-start.1 = (bf16[64,256]{1,0:T(8,128)(2,1)S(1)}, bf16[64,256]{1,0:T(8,128)(2,1)S(1)}, u32[]{:S(2)}, u32[]{:S(2)}) collective-permute-start(bf16[64,256]{1,0:T(8,128)(2,1)S(1)} %get-tuple-element.14), channel_id=1, source_target_pairs={{0,8},{4,12},{8,16},{12,20},{16,24},{20,28},{24,0},{28,4},{1,9},{5... | collective-permute-start | bytes 98312 | tf_op jit(solution)/shard_map/ppermute | solution.py:12
  51.4 8.1 %collective-permute-start = (bf16[64,256]{1,0:T(8,128)(2,1)S(1)}, bf16[64,256]{1,0:T(8,128)(2,1)S(1)}, u32[]{:S(2)}, u32[]{:S(2)}) collective-permute-start(bf16[64,256]{1,0:T(8,128)(2,1)S(1)} %get-tuple-element.11), channel_id=1, source_target_pairs={{0,4},{4,8},{8,12},{12,16},{16,20},{20,24},{24,28},{28,0},{1,5},{5... | collective-permute-start | bytes 98312 | tf_op jit(solution)/shard_map/ppermute | solution.py:12
  57.0 0.7 copy-start.5
  117.7 30.8 %collective-permute-start.4 = (f32[49,256]{1,0:T(8,128)S(1)}, f32[49,256]{1,0:T(8,128)S(1)}, u32[]{:S(2)}, u32[]{:S(2)}) collective-permute-start(f32[49,256]{1,0:T(8,128)S(1)} %slice.37), channel_id=1, source_target_pairs={{0,4},{4,8},{8,12},{12,16},{16,20},{20,24},{24,28},{1,5},{5,9},{9,... | collective-permute-start | bytes 150536
Sparse Core Ops, SparseCore 0:
  17.2 28.9 reduce-scatter.3
Sparse Core Ops, SparseCore 1:
  57.1 89.5 all-reduce.5
where the time goes:
time: 159 us; the launch traced here: 157 us
  blocking collectives  53.1 us (33%)
  waiting for transfers between devices  42.5 us (27%)
  matrix products  17 us (11%)
  between operations  17 us (11%)
  local copies, waits for them, and re-layouts  13.3 us (8%)
  starting transfers between devices  8.91 us (6%)
  other arithmetic  5.67 us (4%)
    unnamed x1, blocking collectives  53.1 us
    unnamed x4, waiting for transfers between devices  24.6 us
    reduce_scatter x1, waiting for transfers between devices, vision(): lax.psum_scatter(partial_value, 'mp', scatter_dimension=1, tiled=True)  17.9 us
    concatenate x1, local copies, waits for them, and re-layouts, per_device(): jnp.concatenate([hidden_rows, ones_column, zero_columns], axis=1)  6.63 us
    dot_general x1, matrix products, vision(): jnp.dot(hidden, fc2_weight, preferred_element_type=jnp.float32)  6.29 us
    dot_general x1, matrix products, per_device(): lax.dot_general(augmented, kv_cotangent, (((0,), (0,)), ((), ())), prefer...  5.07 us
    ppermute x4, starting transfers between devices, shifted(): return lax.ppermute(x, axis, [(i, (i + by) % count) for i in range(count)])  4.45 us
    unnamed x2, starting transfers between devices  4.43 us
  transfers between devices with their start and end apart: 7, of which 2 were waited for; matrix products, arithmetic and copies ran while one was open for 49% of the time, Pallas kernels for 0%

commit v1 on v0

v1 whole, which is shorter than its diff:
```python
import functools

import jax
import jax.numpy as jnp
from jax import lax
from jax.experimental import pallas as pl
from jax.experimental.pallas import tpu as pltpu
from jax.sharding import PartitionSpec as P

MESH = pl.DeviceIdType.MESH
BF = jnp.bfloat16
F32 = jnp.float32


def up(x, m):
    return -(-x // m) * m


def factors(n):
    core = 2 if n % 2 == 0 else 1
    rest = n // core
    inner = max(f for f in range(1, rest + 1) if rest % f == 0 and f * f <= rest)
    return core, inner, rest // inner


def erf_gelu(x):
    return 0.5 * x * (1.0 + lax.erf(x * (0.5**0.5)))


def kernel(
    cfg,
    hid_h, key_h, val_h, vis_h, cot_h, fc1_h, fc2_h,
    gain, beta, fc1_b, fc2_b, scale, counts, offsets,
    key_o, val_o, proj_o, hand_o,
    hid, key, val, vis, cot, fc1, fc2,
    big_k, big_v, big_c,
    cot_send, cot_recv,
    k0, k0r, k1, k1r, k2, k2r,
    v0, v0r, v1, v1r, v2, v2r,
    z_send, z_recv, gath,
    load_sem, cot_ss, cot_rs, z_ss, z_rs,
    k0_s, k0_r, k1_s, k1_r, k2_s, k2_r,
    v0_s, v0_r, v1_s, v1_r, v2_s, v2_r,
    g_s, g_r, f_s, f_r,
):
    n, mp, shard, rows_pad, spread, cap = cfg
    nc, na, nb = factors(n)
    me = lax.axis_index("dp")
    col = lax.axis_index("mp")
    dc = lax.rem(me, nc)
    da = lax.rem(lax.div(me, nc), na)
    db = lax.div(me, nc * na)
    tokens, width = hid.shape
    slots = cot.shape[0]
    kc = key.shape[1]
    fcol = hand_o.shape[1]

    def rank(c, a, b):
        return (b * na + a) * nc + c

    loads = []
    for i, (src, dst) in enumerate(
        ((cot_h, cot), (vis_h, vis), (fc1_h, fc1), (fc2_h, fc2), (hid_h, hid), (key_h, key), (val_h, val))
    ):
        cp = pltpu.make_async_copy(src, dst, load_sem.at[i])
        cp.start()
        loads.append(cp)
    barrier = pltpu.get_barrier_semaphore()
    for j in range(1, n):
        pl.semaphore_signal(barrier, inc=1, device_id={"dp": lax.rem(me + j, n)}, device_id_type=MESH)
    for j in range(1, mp):
        pl.semaphore_signal(barrier, inc=1, device_id={"mp": lax.rem(col + j, mp)}, device_id_type=MESH)

    def remote(src, dst, ss, rs, where):
        cp = pltpu.make_async_remote_copy(
            src_ref=src, dst_ref=dst, send_sem=ss, recv_sem=rs, device_id=where, device_id_type=MESH
        )
        cp.start()
        return cp

    step = 512 if width % 512 == 0 else 128

    loads[0].wait()
    half = 128

    def turn(i, _):
        at = pl.multiple_of(i * step, step)
        for h in range(slots // half):
            piece = cot[h * half : (h + 1) * half, pl.ds(at, step)].astype(F32)
            big_c[h, pl.ds(at, step), :] = piece.T
        return 0

    lax.fori_loop(0, width // step, turn, 0)
    tail = big_c.shape[1] - width
    big_c[:, width:, :] = jnp.zeros((slots // half, tail, half), F32)
    for r in range(n):
        for h in range(slots // half):
            cot_send[r, :, h * half : (h + 1) * half] = big_c[h, r * shard : r * shard + rows_pad, :].astype(BF)
    pl.semaphore_wait(barrier, n - 1 + mp - 1)
    cot_cps = []

    def send_cot():
        for j in range(1, n):
            to = lax.rem(me + j, n)
            cot_cps.append(remote(cot_send.at[to], cot_recv.at[j - 1], cot_ss.at[j - 1], cot_rs.at[j - 1], {"dp": to}))

    send_cot()

    loads[1].wait()
    values = vis[...].astype(F32)
    center = jnp.mean(values, axis=1, keepdims=True)
    cen = values - center
    var = jnp.mean(cen * cen, axis=1, keepdims=True)
    normed = (cen * lax.rsqrt(var + 1e-06) * gain[...] + beta[...]).astype(BF)
    loads[2].wait()
    hidden = erf_gelu(jnp.dot(normed, fc1[...], preferred_element_type=F32) + fc1_b[...]).astype(BF)
    loads[3].wait()

    def feat(i):
        return pl.ds(pl.multiple_of(i * fcol, 128), fcol)

    z_cps = []
    order = sorted(range(1, mp), key=lambda j: abs(j - mp / 2))
    for j in order:
        to = lax.rem(col + j, mp)
        z_send[j - 1] = jnp.dot(hidden, fc2[:, feat(to)], preferred_element_type=F32).astype(BF)
        z_cps.append(remote(z_send.at[j - 1], z_recv.at[j - 1], z_ss.at[j - 1], z_rs.at[j - 1], {"mp": to}))
    own = jnp.dot(hidden, fc2[:, feat(col)], preferred_element_type=F32)

    for cp in loads[4:]:
        cp.wait()
    kv = jnp.concatenate([key[...], val[...]], axis=1)

    def product(i, _):
        at = pl.multiple_of(i * step, step)
        res = lax.dot_general(hid[:, pl.ds(at, step)], kv, (((0,), (0,)), ((), ())), preferred_element_type=F32)
        big_k[pl.ds(at, step), :] = res[:, :kc]
        big_v[pl.ds(at, step), :] = res[:, kc:]
        return 0

    lax.fori_loop(0, width // step, product, 0)
    first = lax.broadcasted_iota(jnp.int32, (tail, kc), 0) == 0
    big_k[width:, :] = jnp.where(first, jnp.sum(key[...].astype(F32), axis=0, keepdims=True), 0.0)
    big_v[width:, :] = jnp.where(first, jnp.sum(val[...].astype(F32), axis=0, keepdims=True), 0.0)
    for r in range(n):
        c, a, b = r % nc, (r // nc) % na, r // (nc * na)
        k0[c, a, b] = big_k[r * shard : r * shard + rows_pad, :].astype(BF)
        v0[c, b, a] = big_v[r * shard : r * shard + rows_pad, :].astype(BF)

    def exchange(buf, got, ss, rs, digit, q, peer_of):
        cps = []
        for j in range(1, q):
            to = lax.rem(digit + j, q)
            cps.append(remote(buf.at[to], got.at[j - 1], ss.at[j - 1], rs.at[j - 1], {"dp": peer_of(to)}))
        return cps

    def added(buf, got, digit, q, at):
        total = buf[(digit,) + at].astype(F32)
        for j in range(1, q):
            total = total + got[(j - 1,) + at].astype(F32)
        return total

    at_c = lambda c: rank(c, da, db)
    at_a = lambda a: rank(dc, a, db)
    at_b = lambda b: rank(dc, da, b)
    s0k = exchange(k0, k0r, k0_s, k0_r, dc, nc, at_c)
    s0v = exchange(v0, v0r, v0_s, v0_r, dc, nc, at_c)

    rows = vis.shape[0]
    images = counts.shape[1]
    place = lax.broadcasted_iota(jnp.int32, (1, rows), 1)
    target = jnp.full((1, rows), -1, jnp.int32)
    start = jnp.int32(0)
    for i in range(images):
        cnt, off = counts[0, i], offsets[0, i]
        before = jnp.int32(0)
        for e in range(i):
            before = before + jnp.where(offsets[0, e] == off, counts[0, e], 0)
        inside = (place >= start) & (place < start + cnt)
        target = jnp.where(inside, (off - 1) * cap + before + place - start, target)
        start = start + cnt
    slot_id = lax.broadcasted_iota(jnp.int32, (spread * cap, rows), 0)
    select = jnp.where(slot_id == target, 1.0, 0.0).astype(BF)

    for cp in s0k:
        cp.wait_recv()
    for a in range(na):
        for b in range(nb):
            k1[a, b] = added(k0, k0r, dc, nc, (a, b)).astype(BF)
    s1k = exchange(k1, k1r, k1_s, k1_r, da, na, at_a)
    for cp in s0v:
        cp.wait_recv()
    for b in range(nb):
        for a in range(na):
            v1[b, a] = added(v0, v0r, dc, nc, (b, a)).astype(BF)
    s1v = exchange(v1, v1r, v1_s, v1_r, db, nb, at_b)

    for cp in z_cps:
        cp.wait_recv()
    summed = own
    for j in range(1, mp):
        summed = summed + z_recv[j - 1].astype(F32)
    encoded = (
        vis[:, feat(col)].astype(F32) + scale[:, feat(col)] * (summed + fc2_b[:, feat(col)])
    ).astype(BF)
    gath[me] = jnp.dot(select, encoded, preferred_element_type=F32).astype(BF)
    chips = n // nc
    chip = lax.div(me, nc)
    g_cps, f_cps = [], []
    for j in range(1, nc):
        f_cps.append(
            remote(gath.at[me], gath.at[me], f_s.at[0, j - 1], f_r.at[0, j - 1], {"dp": at_c(lax.rem(dc + j, nc))})
        )
    for j in range(1, chips):
        to = lax.rem(chip + j, chips) * nc + dc
        g_cps.append(remote(gath.at[me], gath.at[me], g_s.at[j - 1], g_r.at[j - 1], {"dp": to}))

    for cp in s1k:
        cp.wait_recv()
    for b in range(nb):
        k2[b] = added(k1, k1r, da, na, (b,)).astype(BF)
    s2k = exchange(k2, k2r, k2_s, k2_r, db, nb, at_b)
    for cp in s1v:
        cp.wait_recv()
    for a in range(na):
        v2[a] = added(v1, v1r, db, nb, (a,)).astype(BF)
    s2v = exchange(v2, v2r, v2_s, v2_r, da, na, at_a)

    for j in range(1, chips):
        g_cps[j - 1].wait_recv()
        source = lax.rem(chip + chips - j, chips) * nc + dc
        for i in range(1, nc):
            f_cps.append(
                remote(
                    gath.at[source], gath.at[source], f_s.at[j, i - 1], f_r.at[j, i - 1],
                    {"dp": at_c(lax.rem(dc + i, nc))},
                )
            )
    for cp in f_cps:
        cp.wait_recv()

    def received(r):
        parts = []
        for k in range(1, spread + 1):
            source = lax.rem(r + n - k, n)
            parts.append(gath[source, (k - 1) * cap : k * cap, :])
        return jnp.concatenate(parts, axis=0)

    mine = received(me)
    hand_o[...] = mine
    total = jnp.dot(cot_send[me], mine, preferred_element_type=F32)
    for j in range(1, n):
        cot_cps[j - 1].wait_recv()
        total = total + jnp.dot(
            cot_recv[j - 1], received(lax.rem(me + n - j, n)), preferred_element_type=F32
        )
    proj_o[...] = total[:shard]

    for cp in s2k:
        cp.wait_recv()
    key_o[...] = added(k2, k2r, db, nb, ())[:shard]
    for cp in s2v:
        cp.wait_recv()
    val_o[...] = added(v2, v2r, da, na, ())[:shard]
    for cp in cot_cps + z_cps + s0k + s0v + s1k + s1v + s2k + s2v + g_cps + f_cps:
        cp.wait_send()


def per_device(
    n, mp, hidden_rows, key_grad, value_grad, visual_rows, visual_cotangent, norm_gain, norm_bias,
    fc1_weight, fc1_bias, fc2_weight, fc2_bias, layer_scale, token_counts, dest_offsets,
):
    tokens, width = hidden_rows.shape
    spread, cap = visual_cotangent.shape[1:3]
    slots = spread * cap
    shard = (width + n) // n
    rp = up(shard, 16)
    nc, na, nb = factors(n)
    kc = key_grad.shape[1]
    rows, feats = visual_rows.shape
    fcol = feats // mp
    tall = up(max((n - 1) * shard + rp, width + 8), 8)
    any_spec = pl.BlockSpec(memory_space=pl.ANY)
    vm = pl.BlockSpec(memory_space=pltpu.VMEM)
    sm = pl.BlockSpec(memory_space=pltpu.SMEM)
    dma = lambda *s: pltpu.SemaphoreType.DMA(tuple(max(x, 1) for x in s))

    def stages(q1, q2):
        return [
            pltpu.VMEM((nc, q1, q2, rp, kc), BF),
            pltpu.VMEM((max(nc - 1, 1), q1, q2, rp, kc), BF),
            pltpu.VMEM((q1, q2, rp, kc), BF),
            pltpu.VMEM((max(q1 - 1, 1), q2, rp, kc), BF),
            pltpu.VMEM((q2, rp, kc), BF),
            pltpu.VMEM((max(q2 - 1, 1), rp, kc), BF),
        ]

    def stage_sems(q1, q2):
        return [dma(q - 1) for q in (nc, nc, q1, q1, q2, q2)]

    outs = pl.pallas_call(
        functools.partial(kernel, (n, mp, shard, rp, spread, cap)),
        out_shape=(
            jax.ShapeDtypeStruct((shard, kc), F32),
            jax.ShapeDtypeStruct((shard, kc), F32),
            jax.ShapeDtypeStruct((shard, fcol), F32),
            jax.ShapeDtypeStruct((slots, fcol), BF),
        ),
        in_specs=[any_spec] * 7 + [vm] * 5 + [sm] * 2,
        out_specs=(vm, vm, vm, vm),
        scratch_shapes=[
            pltpu.VMEM(x.shape, BF)
            for x in (hidden_rows, key_grad, value_grad, visual_rows)
        ]
        + [
            pltpu.VMEM((slots, width), BF),
            pltpu.VMEM(fc1_weight.shape, BF),
            pltpu.VMEM(fc2_weight.shape, BF),
            pltpu.VMEM((tall, kc), F32),
            pltpu.VMEM((tall, kc), F32),
            pltpu.VMEM((slots // 128, tall, 128), F32),
            pltpu.VMEM((n, rp, slots), BF),
            pltpu.VMEM((n - 1, rp, slots), BF),
        ]
        + stages(na, nb)
        + stages(nb, na)
        + [
            pltpu.VMEM((mp - 1, rows, fcol), BF),
            pltpu.VMEM((mp - 1, rows, fcol), BF),
            pltpu.VMEM((n, slots, fcol), BF),
            dma(7), dma(n - 1), dma(n - 1), dma(mp - 1), dma(mp - 1),
        ]
        + stage_sems(na, nb)
        + stage_sems(nb, na)
        + [dma(n // nc - 1), dma(n // nc - 1), dma(n // nc, nc - 1), dma(n // nc, nc - 1)],
        compiler_params=pltpu.CompilerParams(
            collective_id=0, has_side_effects=True, vmem_limit_bytes=60 * 1024 * 1024
        ),
    )(
        hidden_rows, key_grad, value_grad, visual_rows, visual_cotangent.reshape(slots, width),
        fc1_weight, fc2_weight, norm_gain[None], norm_bias[None], fc1_bias[None], fc2_bias[None],
        layer_scale[None], token_counts, dest_offsets,
    )
    return outs[0], outs[1], outs[2], outs[3].reshape(1, spread, cap, fcol)


def solution(mesh):
    placed = (
        P("dp", None), P("dp", "mp"), P("dp", "mp"), P("dp", None), P("dp", None, None, None),
        P(), P(), P(None, "mp"), P("mp"), P("mp", None), P(), P(), P("dp", None), P("dp", None),
    )
    return jax.shard_map(
        functools.partial(per_device, mesh.shape["dp"], mesh.shape["mp"]),
        mesh=mesh,
        in_specs=placed,
        out_specs=(P("dp", "mp"), P("dp", "mp"), P("dp", "mp"), P("dp", None, None, "mp")),
        check_vma=False,
    )
```

time: 159 us -> 51.7 us (0.33)
  blocking collectives: 53.1 us -> 0 us
  Pallas kernels: 0 us -> 44.1 us
  waiting for transfers between devices: 42.5 us -> 0 us
  matrix products: 17 us -> 0 us
  between operations: 17 us -> 0.65 us
  starting transfers between devices: 8.91 us -> 0 us
  local copies, waits for them, and re-layouts: 13.3 us -> 6.68 us
  other arithmetic: 5.67 us -> 0 us
    unnamed x1 -> x0, blocking collectives: 53.1 us -> none
    pallas_call x0 -> x1, Pallas kernels: none -> 44.1 us  [per_device(): pl.pallas_call(functools.partial(kernel, (n, mp, shard, rp, spread, cap))...]
    unnamed x4 -> x0, waiting for transfers between devices: 24.6 us -> none
    reduce_scatter x1 -> x0, waiting for transfers between devices: 17.9 us -> none  [vision(): lax.psum_scatter(partial_value, 'mp', scatter_dimension=1, tiled=True)]
    dot_general x4 -> x0, matrix products: 17 us -> none  [the longest x1 6.29 us: vision(): jnp.dot(hidden, fc2_weight, preferred_element_type=jnp.float32)]
    concatenate x1 -> x0, local copies, waits for them, and re-layouts: 6.63 us -> none  [per_device(): jnp.concatenate([hidden_rows, ones_column, zero_columns], axis=1)]
    ppermute x4 -> x0, starting transfers between devices: 4.45 us -> none  [shifted(): return lax.ppermute(x, axis, [(i, (i + by) % count) for i in range(count)])]
    unnamed x2 -> x0, starting transfers between devices: 4.43 us -> none
  transfers between devices with their start and end apart: 7 -> 0, of which waited for: 2 -> 0; matrix products, arithmetic and copies ran while one was open for 49% -> 0% of each run, Pallas kernels for 0% -> 0%
where the time goes in v1:
time: 51.7 us; the launch traced here: 51.4 us
  Pallas kernels  44.1 us (85%)
  local copies, waits for them, and re-layouts  6.68 us (13%)
  between operations  0.65 us (1%)
    pallas_call x1, Pallas kernels, per_device(): pl.pallas_call(functools.partial(kernel, (n, mp, shard, rp, spread, cap))...  44.1 us
    unnamed x4, local copies, waits for them, and re-layouts  6.68 us

profile of v1, /device:TPU:1, one launch (start us, length us, event | category | flops | bytes accessed | tf_op | source)
XLA Modules:
  0.0 51.4 jit_solution(12081390647545586662)
XLA Ops:
  0.6 44.1 %shard_map.165 = (f32[449,128]{1,0:T(8,128)}, f32[449,128]{1,0:T(8,128)}, f32[449,256]{1,0:T(8,128)}, bf16[256,256]{1,0:T(8,128)(2,1)}) custom-call(bf16[512,3584]{1,0:T(8,128)(2,1)} %hid_h.1, bf16[512,128]{1,0:T(8,128)(2,1)} %key_h.1, bf16[512,128]{1,0:T(8,128)(2,1)} %val_h.1, bf16[256,1024]{1,0:T(8,128)(2,1)} %vis_h.1, bf16[256,3584]{1,0:T(8,128)(2,1)} %bitcast.7, ...), custom_call_target="tpu_custom_call" | custom-call | tf_op jit(solution)/shard_map/pallas_call | solution.py:301
  44.8 1.6 %copy.22 = f32[449,128]{1,0:T(8,128)} copy(f32[449,128]{1,0:T(8,128)} %get-tuple-element.16) | data formatting | bytes 459776
  46.4 1.6 %copy.23 = f32[449,128]{1,0:T(8,128)} copy(f32[449,128]{1,0:T(8,128)} %get-tuple-element.17) | data formatting | bytes 459776
  48.0 1.8 %copy.24 = f32[449,256]{1,0:T(8,128)} copy(f32[449,256]{1,0:T(8,128)} %get-tuple-element.18) | data formatting | bytes 919552
  49.9 1.6 %copy.25 = bf16[1,4,64,256]{3,2,1,0:T(8,128)(2,1)} copy(bf16[1,4,64,256]{3,2,1,0:T(8,128)(2,1)} %bitcast.8) | data formatting | bytes 262144

commit v2 on v1

--- a/solution.py
+++ b/solution.py
@@ -264,6 +264,12 @@
     val_o[...] = added(v2, v2r, da, na, ())[:shard]
     for cp in cot_cps + z_cps + s0k + s0v + s1k + s1v + s2k + s2v + g_cps + f_cps:
         cp.wait_send()
+
+
+def finish(*refs):
+    half = len(refs) // 2
+    for src, dst in zip(refs[:half], refs[half:]):
+        dst[...] = src[...]
 
 
 def per_device(
@@ -341,6 +347,12 @@
         fc1_weight, fc2_weight, norm_gain[None], norm_bias[None], fc1_bias[None], fc2_bias[None],
         layer_scale[None], token_counts, dest_offsets,
     )
+    outs = pl.pallas_call(
+        finish,
+        out_shape=tuple(jax.ShapeDtypeStruct(x.shape, x.dtype) for x in outs),
+        in_specs=[vm] * 4,
+        out_specs=(vm,) * 4,
+    )(*outs)
     return outs[0], outs[1], outs[2], outs[3].reshape(1, spread, cap, fcol)
 
 

time: 51.7 us -> 47.2 us (0.913)
  local copies, waits for them, and re-layouts: 6.68 us -> 0 us
  Pallas kernels: 44.1 us -> 46.4 us
    unnamed x4 -> x0, local copies, waits for them, and re-layouts: 6.68 us -> none
    pallas_call x0 -> x1, Pallas kernels: none -> 2.26 us  [per_device(): pl.pallas_call(finish, out_shape=tuple((jax.ShapeDtypeStruct(x.shape, x.d...]
where the time goes in v2:
time: 47.2 us; the launch traced here: 47 us
  Pallas kernels  46.4 us (98%)
  between operations  0.64 us (1%)
    pallas_call x1, Pallas kernels, per_device(): pl.pallas_call(functools.partial(kernel, (n, mp, shard, rp, spread, cap))...  44.1 us
    pallas_call x1, Pallas kernels, per_device(): pl.pallas_call(finish, out_shape=tuple((jax.ShapeDtypeStruct(x.shape, x.d...  2.26 us

profile of v2, /device:TPU:1, one launch (start us, length us, event | category | flops | bytes accessed | tf_op | source)
XLA Modules:
  0.0 47.0 jit_solution(11370223513239082711)
XLA Ops:
  0.6 44.1 %shard_map.165 = (f32[449,128]{1,0:T(8,128)}, f32[449,128]{1,0:T(8,128)}, f32[449,256]{1,0:T(8,128)}, bf16[256,256]{1,0:T(8,128)(2,1)}) custom-call(bf16[512,3584]{1,0:T(8,128)(2,1)} %hid_h.1, bf16[512,128]{1,0:T(8,128)(2,1)} %key_h.1, bf16[512,128]{1,0:T(8,128)(2,1)} %val_h.1, bf16[256,1024]{1,0:T(8,128)(2,1)} %vis_h.1, bf16[256,3584]{1,0:T(8,128)(2,1)} %bitcast.7, ...), custom_call_target="tpu_custom_call" | custom-call | tf_op jit(solution)/shard_map/pallas_call | solution.py:307
  44.8 2.3 %shard_map.166 = (f32[449,128]{1,0:T(8,128)}, f32[449,128]{1,0:T(8,128)}, f32[449,256]{1,0:T(8,128)}, bf16[256,256]{1,0:T(8,128)(2,1)}) custom-call(f32[449,128]{1,0:T(8,128)} %get-tuple-element.12.refs_0_, f32[449,128]{1,0:T(8,128)} %get-tuple-element.13.refs_1_, f32[449,256]{1,0:T(8,128)} %get-tuple-element.14.refs_2_, ...), custom_call_target="tpu_custom_call" | custom-call | tf_op jit(solution)/shard_map/pallas_call | solution.py:350
